TPU v7x, 32 devices: a whole 2x2x4 slice. The times are simulated.
32 devices in a mesh: expert: 4 (over y, core), shard: 8 (over z, x).
Axes of the slice: x: 2, y: 2, z: 4, core: 2. Of those that a mesh axis runs over, the one named last changes fastest.
Arguments:
- master_gate: float32 [128, 2048, 768], P('expert', 'shard'), may hold values from -0.125 to 0.125
- second_gate: bfloat16 [128, 2048, 768], P('expert', 'shard'), may hold values from -0.0625 to 0.0625
- master_up: float32 [128, 2048, 768], P('expert', 'shard'), may hold values from -0.125 to 0.125
- second_up: bfloat16 [128, 2048, 768], P('expert', 'shard'), may hold values from -0.0625 to 0.0625
- router_weight: float32 [2048, 128], P('shard', 'expert'), may hold values from -0.125 to 0.125
- router_gain: float32 [2048], P('shard'), may hold values from 0.25 to 1.75
Outputs:
- final_gate: bfloat16 [128, 768, 2048], P('expert', 'shard')
- final_up: bfloat16 [128, 768, 2048], P('expert', 'shard')
- serve_router: bfloat16 [2048, 128], replicated
All inputs are finite; a program needn't handle non-finite values.
Results may differ from a plain program's by a relative error of at most 0.001.
Values may be sent and summed in bfloat16 or wider, within the bound.
A program may use at most 192 MiB of HBM per device.

v0:
```python
import jax
import jax.numpy as jnp
from jax import lax
from jax.sharding import PartitionSpec as P


def per_device(master_gate, second_gate, master_up, second_up, router_weight, router_gain):
    merged_gate = master_gate + second_gate.astype(jnp.float32)
    merged_up = master_up + second_up.astype(jnp.float32)
    narrow_gate, narrow_up = (merged_gate.astype(jnp.bfloat16), merged_up.astype(jnp.bfloat16))
    final_gate, final_up = (
        lax.all_to_all(narrow_gate, "shard", split_axis=2, concat_axis=1, tiled=True),
        lax.all_to_all(narrow_up, "shard", split_axis=2, concat_axis=1, tiled=True),
    )
    final_gate = jnp.transpose(final_gate, (0, 2, 1))
    final_up = jnp.transpose(final_up, (0, 2, 1))
    part_router = (router_weight * router_gain[:, None]).astype(jnp.bfloat16)
    row_router = lax.all_gather(part_router, "shard", axis=0, tiled=True)
    serve_router = lax.all_gather(row_router, "expert", axis=1, tiled=True)
    return (final_gate, final_up, serve_router)


def solution(mesh):
    placed = (
        P("expert", "shard", None),
        P("expert", "shard", None),
        P("expert", "shard", None),
        P("expert", "shard", None),
        P("shard", "expert"),
        P("shard"),
    )
    return jax.shard_map(
        per_device,
        mesh=mesh,
        in_specs=placed,
        out_specs=(P("expert", "shard", None), P("expert", "shard", None), P()),
        check_vma=False,
    )
```

profile of v0, /device:TPU:0, one launch (start us, length us, event | category | flops | bytes accessed | tf_op | source)
XLA Modules:
  0.0 713.1 jit_solution(3689968632232905963)
XLA Ops:
  0.6 25.0 %copy.25 = f32[32,256,768]{1,0,2:T(8,128)} copy(f32[32,256,768]{2,1,0:T(8,128)} %param.6) | data formatting | bytes 50331648 | tf_op args[0]
  25.7 16.9 %copy.24 = bf16[32,256,768]{1,0,2:T(8,128)(2,1)} copy(bf16[32,256,768]{2,1,0:T(8,128)(2,1)} %param.7) | data formatting | bytes 25165824 | tf_op args[1]
  42.5 17.3 %add_convert_fusion.1 = bf16[32,256,768]{1,0,2:T(8,128)(2,1)} fusion(f32[32,256,768]{1,0,2:T(8,128)} %copy.25, bf16[32,256,768]{1,0,2:T(8,128)(2,1)} %copy.24), kind=kLoop, calls=%fused_computation.1 | loop fusion | flops 18874368 | bytes 50331648 | tf_op jit(solution)/shard_map/convert_element_type | solution.py:10
  59.8 7.3 %all-to-all-start = ((bf16[32,256,768]{1,0,2:T(8,128)(2,1)}), bf16[32,256,768]{1,0,2:T(8,128)(2,1)}, u32[]{:S(2)}, u32[]{:S(2)}) async-start(bf16[32,256,768]{1,0,2:T(8,128)(2,1)} %add_convert_fusion.1), calls=%async_computation | async-start | bytes 25165824 | tf_op jit(solution)/shard_map/all_to_all | solution.py:12
  67.1 25.0 %copy.29 = f32[32,256,768]{1,0,2:T(8,128)} copy(f32[32,256,768]{2,1,0:T(8,128)} %param.8) | data formatting | bytes 50331648 | tf_op args[2]
  92.2 16.9 %copy.28 = bf16[32,256,768]{1,0,2:T(8,128)(2,1)} copy(bf16[32,256,768]{2,1,0:T(8,128)(2,1)} %param.9) | data formatting | bytes 25165824 | tf_op args[3]
  109.0 17.3 %add_convert_fusion = bf16[32,256,768]{1,0,2:T(8,128)(2,1)} fusion(f32[32,256,768]{1,0,2:T(8,128)} %copy.29, bf16[32,256,768]{1,0,2:T(8,128)(2,1)} %copy.28), kind=kLoop, calls=%fused_computation | loop fusion | flops 18874368 | bytes 50331648 | tf_op jit(solution)/shard_map/convert_element_type | solution.py:10
  126.3 0.0 copy-start
  126.3 0.0 copy-start.1
  126.3 213.9 %all-to-all-done = bf16[32,256,768]{1,0,2:T(8,128)(2,1)} async-done(((bf16[32,256,768]{1,0,2:T(8,128)(2,1)}), bf16[32,256,768]{1,0,2:T(8,128)(2,1)}, u32[]{:S(2)}, u32[]{:S(2)}) %all-to-all-start) | async-done | bytes 12582944 | tf_op jit(solution)/shard_map/all_to_all | solution.py:12
  340.2 5.3 all-to-all-start.1
  345.5 0.0 copy-done
  345.5 0.0 copy-done.1
  345.6 292.2 %all_gather.6 = bf16[2048,32]{0,1:T(8,128)(2,1)S(1)} all-gather(bf16[256,32]{0,1:T(8,128)(2,1)S(1)} %multiply_convert_fusion), channel_id=1, replica_groups=mesh['expert'=4,'shard'=8] {'shard'}, dimensions={0}, use_global_device_ids=true | all-gather | bytes 147456 | tf_op jit(solution)/shard_map/all_gather | solution.py:18
  637.8 7.2 %all_gather.7 = bf16[2048,128]{0,1:T(8,128)(2,1)S(1)} all-gather(bf16[2048,32]{0,1:T(8,128)(2,1)S(1)} %all_gather.6), channel_id=1, replica_groups=mesh['expert'=4,'shard'=8] {'expert'}, dimensions={1}, use_global_device_ids=true | all-gather | bytes 655360 | tf_op jit(solution)/shard_map/all_gather | solution.py:19
  645.0 1.0 copy.32
  646.0 14.1 %copy.27 = bf16[32,8,256,96]{2,1,3,0:T(8,128)(2,1)} copy(bf16[32,8,256,96]{2,0,3,1:T(8,128)(2,1)} %bitcast.2) | data formatting | bytes 25165824 | tf_op jit(solution)/shard_map/all_to_all | solution.py:12
  660.0 19.5 %all_to_all.29 = bf16[32,2048,96]{1,2,0:T(8,128)(2,1)} reshape(bf16[32,8,256,96]{2,1,3,0:T(8,128)(2,1)} %copy.27) | data formatting | bytes 25165824 | tf_op jit(solution)/shard_map/all_to_all | solution.py:12
  679.5 0.0 all-to-all-done.1
  679.5 14.1 %copy.31 = bf16[32,8,256,96]{2,1,3,0:T(8,128)(2,1)} copy(bf16[32,8,256,96]{2,0,3,1:T(8,128)(2,1)} %bitcast.6) | data formatting | bytes 25165824 | tf_op jit(solution)/shard_map/all_to_all | solution.py:13
  693.6 19.5 %all_to_all.33 = bf16[32,2048,96]{1,2,0:T(8,128)(2,1)} reshape(bf16[32,8,256,96]{2,1,3,0:T(8,128)(2,1)} %copy.31) | data formatting | bytes 25165824 | tf_op jit(solution)/shard_map/all_to_all | solution.py:13
  (1 shorter events, 0.0 us)
Async XLA Ops:
  59.8 280.3 %all-to-all-start = ((bf16[32,256,768]{1,0,2:T(8,128)(2,1)}), bf16[32,256,768]{1,0,2:T(8,128)(2,1)}, u32[]{:S(2)}, u32[]{:S(2)}) async-start(bf16[32,256,768]{1,0,2:T(8,128)(2,1)} %add_convert_fusion.1), calls=%async_computation | async-start | bytes 25165824 | tf_op jit(solution)/shard_map/all_to_all | solution.py:12
  126.3 219.2 %copy-start = (f32[256,32]{0,1:T(8,128)S(1)}, f32[256,32]{0,1:T(8,128)}, u32[]{:S(2)}) copy-start(f32[256,32]{0,1:T(8,128)} %param.10) | copy-start | bytes 98308
  126.3 219.2 %copy-start.1 = (f32[256]{0:T(256)S(1)}, f32[256]{0:T(256)}, u32[]{:S(2)}) copy-start(f32[256]{0:T(256)} %param.11) | copy-start | bytes 3076
  340.2 339.3 %all-to-all-start.1 = ((bf16[32,256,768]{1,0,2:T(8,128)(2,1)}), bf16[32,256,768]{1,0,2:T(8,128)(2,1)}, u32[]{:S(2)}, u32[]{:S(2)}) async-start(bf16[32,256,768]{1,0,2:T(8,128)(2,1)} %add_convert_fusion), calls=%async_computation.1 | async-start | bytes 25165824 | tf_op jit(solution)/shard_map/all_to_all | solution.py:13
where the time goes:
time: 716 us; the launch traced here: 713 us
  blocking collectives  299 us (42%)
  waiting for transfers between devices  214 us (30%)
  local copies, waits for them, and re-layouts  152 us (21%)
  other arithmetic  34.6 us (5%)
  starting transfers between devices  12.6 us (2%)
    all_gather x1, blocking collectives, per_device(): row_router = lax.all_gather(part_router, 'shard', axis=0, tiled=True)  292 us
    all_to_all x1, waiting for transfers between devices, per_device(): lax.all_to_all(narrow_gate, 'shard', split_axis=2, concat_axis=1, tiled=T...  214 us
    unnamed x9, local copies, waits for them, and re-layouts  84.8 us
    all_to_all x2, local copies, waits for them, and re-layouts, per_device(): lax.all_to_all(narrow_up, 'shard', split_axis=2, concat_axis=1, tiled=True)  33.6 us
    all_to_all x2, local copies, waits for them, and re-layouts, per_device(): lax.all_to_all(narrow_gate, 'shard', split_axis=2, concat_axis=1, tiled=T...  33.5 us
    convert_element_type x1, other arithmetic, per_device(): merged_gate.astype(jnp.bfloat16)  17.3 us
    convert_element_type x1, other arithmetic, per_device(): merged_up.astype(jnp.bfloat16)  17.3 us
  transfers between devices with their start and end apart: 2, of which 1 were waited for; matrix products, arithmetic and copies ran while one was open for 10% of the time, Pallas kernels for 0%

commit v1 on v0

--- a/solution.py
+++ b/solution.py
@@ -2,6 +2,11 @@
 import jax.numpy as jnp
 from jax import lax
 from jax.sharding import PartitionSpec as P
+
+
+def gathered_along(x, axis, dim):
+    shards = lax.all_gather(x, axis)
+    return jnp.concatenate(shards, axis=dim)
 
 
 def per_device(master_gate, second_gate, master_up, second_up, router_weight, router_gain):
@@ -16,7 +21,7 @@
     final_up = jnp.transpose(final_up, (0, 2, 1))
     part_router = (router_weight * router_gain[:, None]).astype(jnp.bfloat16)
     row_router = lax.all_gather(part_router, "shard", axis=0, tiled=True)
-    serve_router = lax.all_gather(row_router, "expert", axis=1, tiled=True)
+    serve_router = gathered_along(row_router, "expert", 1)
     return (final_gate, final_up, serve_router)
 
 

time: 716 us -> 717 us (level)
  no operation moved by 1% of the time
where the time goes in v1:
time: 717 us; the launch traced here: 714 us
  blocking collectives  299 us (42%)
  waiting for transfers between devices  214 us (30%)
  local copies, waits for them, and re-layouts  153 us (21%)
  other arithmetic  34.6 us (5%)
  starting transfers between devices  12.6 us (2%)
    all_gather x1, blocking collectives, per_device(): row_router = lax.all_gather(part_router, 'shard', axis=0, tiled=True)  292 us
    all_to_all x1, waiting for transfers between devices, per_device(): lax.all_to_all(narrow_gate, 'shard', split_axis=2, concat_axis=1, tiled=T...  214 us
    unnamed x9, local copies, waits for them, and re-layouts  84.8 us
    all_to_all x2, local copies, waits for them, and re-layouts, per_device(): lax.all_to_all(narrow_up, 'shard', split_axis=2, concat_axis=1, tiled=True)  33.6 us
    all_to_all x2, local copies, waits for them, and re-layouts, per_device(): lax.all_to_all(narrow_gate, 'shard', split_axis=2, concat_axis=1, tiled=T...  33.5 us
    convert_element_type x1, other arithmetic, per_device(): merged_gate.astype(jnp.bfloat16)  17.3 us
    convert_element_type x1, other arithmetic, per_device(): merged_up.astype(jnp.bfloat16)  17.3 us
  transfers between devices with their start and end apart: 2, of which 1 were waited for; matrix products, arithmetic and copies ran while one was open for 10% of the time, Pallas kernels for 0%

profile of v1, /device:TPU:0, one launch (start us, length us, event | category | flops | bytes accessed | tf_op | source)
XLA Modules:
  0.0 713.7 jit_solution(1268818955185201082)
XLA Ops:
  0.6 25.0 %copy.26 = f32[32,256,768]{1,0,2:T(8,128)} copy(f32[32,256,768]{2,1,0:T(8,128)} %param.6) | data formatting | bytes 50331648 | tf_op args[0]
  25.7 16.9 %copy.25 = bf16[32,256,768]{1,0,2:T(8,128)(2,1)} copy(bf16[32,256,768]{2,1,0:T(8,128)(2,1)} %param.7) | data formatting | bytes 25165824 | tf_op args[1]
  42.5 17.3 %add_convert_fusion.1 = bf16[32,256,768]{1,0,2:T(8,128)(2,1)} fusion(f32[32,256,768]{1,0,2:T(8,128)} %copy.26, bf16[32,256,768]{1,0,2:T(8,128)(2,1)} %copy.25), kind=kLoop, calls=%fused_computation.1 | loop fusion | flops 18874368 | bytes 50331648 | tf_op jit(solution)/shard_map/convert_element_type | solution.py:15
  59.8 7.3 %all-to-all-start = ((bf16[32,256,768]{1,0,2:T(8,128)(2,1)}), bf16[32,256,768]{1,0,2:T(8,128)(2,1)}, u32[]{:S(2)}, u32[]{:S(2)}) async-start(bf16[32,256,768]{1,0,2:T(8,128)(2,1)} %add_convert_fusion.1), calls=%async_computation | async-start | bytes 25165824 | tf_op jit(solution)/shard_map/all_to_all | solution.py:17
  67.1 25.0 %copy.30 = f32[32,256,768]{1,0,2:T(8,128)} copy(f32[32,256,768]{2,1,0:T(8,128)} %param.8) | data formatting | bytes 50331648 | tf_op args[2]
  92.2 16.9 %copy.29 = bf16[32,256,768]{1,0,2:T(8,128)(2,1)} copy(bf16[32,256,768]{2,1,0:T(8,128)(2,1)} %param.9) | data formatting | bytes 25165824 | tf_op args[3]
  109.0 17.3 %add_convert_fusion = bf16[32,256,768]{1,0,2:T(8,128)(2,1)} fusion(f32[32,256,768]{1,0,2:T(8,128)} %copy.30, bf16[32,256,768]{1,0,2:T(8,128)(2,1)} %copy.29), kind=kLoop, calls=%fused_computation | loop fusion | flops 18874368 | bytes 50331648 | tf_op jit(solution)/shard_map/convert_element_type | solution.py:15
  126.3 0.0 copy-start
  126.3 0.0 copy-start.1
  126.3 213.9 %all-to-all-done = bf16[32,256,768]{1,0,2:T(8,128)(2,1)} async-done(((bf16[32,256,768]{1,0,2:T(8,128)(2,1)}), bf16[32,256,768]{1,0,2:T(8,128)(2,1)}, u32[]{:S(2)}, u32[]{:S(2)}) %all-to-all-start) | async-done | bytes 12582944 | tf_op jit(solution)/shard_map/all_to_all | solution.py:17
  340.2 5.3 all-to-all-start.1
  345.5 0.0 copy-done
  345.5 0.0 copy-done.1
  345.6 292.2 %all_gather.9 = bf16[2048,32]{0,1:T(8,128)(2,1)S(1)} all-gather(bf16[256,32]{0,1:T(8,128)(2,1)S(1)} %multiply_convert_fusion), channel_id=1, replica_groups=mesh['expert'=4,'shard'=8] {'shard'}, dimensions={0}, use_global_device_ids=true | all-gather | bytes 147456 | tf_op jit(solution)/shard_map/all_gather | solution.py:23
  637.8 7.2 %all-gather = bf16[8192,32]{0,1:T(8,128)(2,1)S(1)} all-gather(bf16[2048,32]{0,1:T(8,128)(2,1)S(1)} %all_gather.9), channel_id=2, replica_groups=mesh['expert'=4,'shard'=8] {'expert'}, dimensions={0}, use_global_device_ids=true | all-gather | bytes 655360 | tf_op jit(solution)/shard_map/all_gather | solution.py:8
  645.0 0.4 reshape.15
  645.3 0.3 copy.33
  645.6 1.0 copy.34
  646.6 14.1 %copy.28 = bf16[32,8,256,96]{2,1,3,0:T(8,128)(2,1)} copy(bf16[32,8,256,96]{2,0,3,1:T(8,128)(2,1)} %bitcast.2) | data formatting | bytes 25165824 | tf_op jit(solution)/shard_map/all_to_all | solution.py:17
  660.7 19.5 %all_to_all.29 = bf16[32,2048,96]{1,2,0:T(8,128)(2,1)} reshape(bf16[32,8,256,96]{2,1,3,0:T(8,128)(2,1)} %copy.28) | data formatting | bytes 25165824 | tf_op jit(solution)/shard_map/all_to_all | solution.py:17
  680.2 0.0 all-to-all-done.1
  680.2 14.1 %copy.32 = bf16[32,8,256,96]{2,1,3,0:T(8,128)(2,1)} copy(bf16[32,8,256,96]{2,0,3,1:T(8,128)(2,1)} %bitcast.6) | data formatting | bytes 25165824 | tf_op jit(solution)/shard_map/all_to_all | solution.py:18
  694.3 19.5 %all_to_all.33 = bf16[32,2048,96]{1,2,0:T(8,128)(2,1)} reshape(bf16[32,8,256,96]{2,1,3,0:T(8,128)(2,1)} %copy.32) | data formatting | bytes 25165824 | tf_op jit(solution)/shard_map/all_to_all | solution.py:18
  (1 shorter events, 0.0 us)
Async XLA Ops:
  59.8 280.3 %all-to-all-start = ((bf16[32,256,768]{1,0,2:T(8,128)(2,1)}), bf16[32,256,768]{1,0,2:T(8,128)(2,1)}, u32[]{:S(2)}, u32[]{:S(2)}) async-start(bf16[32,256,768]{1,0,2:T(8,128)(2,1)} %add_convert_fusion.1), calls=%async_computation | async-start | bytes 25165824 | tf_op jit(solution)/shard_map/all_to_all | solution.py:17
  126.3 219.2 %copy-start = (f32[256,32]{0,1:T(8,128)S(1)}, f32[256,32]{0,1:T(8,128)}, u32[]{:S(2)}) copy-start(f32[256,32]{0,1:T(8,128)} %param.10) | copy-start | bytes 98308
  126.3 219.2 %copy-start.1 = (f32[256]{0:T(256)S(1)}, f32[256]{0:T(256)}, u32[]{:S(2)}) copy-start(f32[256]{0:T(256)} %param.11) | copy-start | bytes 3076
  340.2 340.0 %all-to-all-start.1 = ((bf16[32,256,768]{1,0,2:T(8,128)(2,1)}), bf16[32,256,768]{1,0,2:T(8,128)(2,1)}, u32[]{:S(2)}, u32[]{:S(2)}) async-start(bf16[32,256,768]{1,0,2:T(8,128)(2,1)} %add_convert_fusion), calls=%async_computation.1 | async-start | bytes 25165824 | tf_op jit(solution)/shard_map/all_to_all | solution.py:18
